TPU v7x, 32 devices: a whole 2x2x4 slice. The times are simulated.
32 devices in a mesh: grp: 8 (over z, x), tbl: 4 (over y, core).
Axes of the slice: x: 2, y: 2, z: 4, core: 2. Of those that a mesh axis runs over, the one named last changes fastest.
Arguments:
- next_ids: int32 [4096, 224], P(('grp', 'tbl')), may hold values from 0 to 6143
- next_lengths: int32 [4096, 26], P(('grp', 'tbl')), may hold values from 1 to 8
- slot_of_table: int32 [26], replicated, may hold values from 0 to 27, as said below
- tables: bfloat16 [28, 6144, 128], P('tbl'), may hold values from -2.5 to 2.5
- cross_input: bfloat16 [4096, 3456], P(('grp', 'tbl')), may hold values from -6 to 6
- cotangent: bfloat16 [4096, 3456], P(('grp', 'tbl')), may hold values from -6 to 6
- up_weight: bfloat16 [256, 3456], replicated, may hold values from -0.375 to 0.375
- down_weight: bfloat16 [3456, 256], replicated, may hold values from -0.109375 to 0.109375
Outputs:
- next_embedded: bfloat16 [4096, 3328], P(('grp', 'tbl'))
- grad_up: float32 [256, 3456], P('tbl', 'grp')
- grad_down: float32 [3456, 256], P('grp', 'tbl')
Inputs may be any that keep to these rules, and one draw needn't show every extreme that they name: `next_ids`: entry 8 * s + k of an example's row is the k-th id of the bag held in slot s; entries with k at or past the bag's length, and all entries of slots that hold no table, are padding. `slot_of_table`: distinct slots; owner o along tbl holds slots o * 7 to o * 7 + 6, so an owner holds up to 7 tables and some owner holds exactly 7.
All inputs are finite; a program needn't handle non-finite values.
Results may differ from a plain program's by a relative error of at most 0.0049.
Values may be sent and summed in bfloat16 or wider, within the bound.
A program may use at most 128 MiB of HBM per device.

v0:
```python
import math

import jax
import jax.numpy as jnp
from jax import lax
from jax.sharding import PartitionSpec as P


def pool_rows(table_flat, ids, lens, slots, maxlen):
    count = ids.shape[0]
    width = table_flat.shape[1]
    rows_each = table_flat.shape[0] // slots
    ids_three = ids.reshape(count, slots, maxlen)
    offset = lax.broadcasted_iota(jnp.int32, (1, slots, 1), 1) * rows_each
    picked = jnp.take(table_flat, (ids_three + offset).reshape(-1), axis=0).reshape(
        count, slots, maxlen, width
    )
    keep = lax.broadcasted_iota(jnp.int32, (count, slots, maxlen), 2) < lens[:, :, None]
    masked = jnp.where(keep[..., None], picked, jnp.zeros((), picked.dtype))
    pooled = jnp.sum(masked, axis=2, dtype=jnp.float32)
    return pooled.astype(jnp.bfloat16).reshape(count, slots * width)


def on_device(
    next_ids, next_lengths, slot_of_table, tables, cross_input, cotangent, up_weight, down_weight
):
    batch = next_ids.shape[0]
    owners = lax.axis_size("tbl")
    slots = tables.shape[0]
    slots_all = slots * owners
    maxlen = next_ids.shape[1] // slots_all
    width = tables.shape[2]
    feats = slot_of_table.shape[0]
    hit = (slot_of_table[:, None] == lax.broadcasted_iota(jnp.int32, (1, slots_all), 1)).astype(
        jnp.int32
    )
    slot_lengths = jnp.sum(next_lengths[:, :, None] * hit[None, :, :], axis=1)
    block = 64
    items = batch // block
    id_blocks = next_ids.reshape(items, block, slots_all * maxlen)
    len_blocks = slot_lengths.reshape(items, block, slots_all)
    table_flat = tables.reshape(slots * tables.shape[1], width)
    got_ids = lax.all_to_all(id_blocks, "tbl", split_axis=2, concat_axis=1, tiled=True)
    got_lens = lax.all_to_all(len_blocks, "tbl", split_axis=2, concat_axis=1, tiled=True)
    pooled = lax.map(
        lambda pair: pool_rows(table_flat, pair[0], pair[1], slots, maxlen), (got_ids, got_lens)
    )
    returned = lax.all_to_all(pooled, "tbl", split_axis=1, concat_axis=2, tiled=True)
    by_slot = returned.reshape(batch, slots_all, width)
    next_embedded = jnp.take(by_slot, slot_of_table, axis=1).reshape(batch, feats * width)
    low = jnp.dot(cross_input, down_weight, preferred_element_type=jnp.float32).astype(jnp.bfloat16)
    dz = (cotangent.astype(jnp.float32) * cross_input.astype(jnp.float32)).astype(jnp.bfloat16)
    dlow = jnp.dot(dz, up_weight.T, preferred_element_type=jnp.float32).astype(jnp.bfloat16)
    total = batch * lax.axis_size("grp") * owners
    factor = 1.0 / math.sqrt(total)
    part_up = jnp.dot(low.T, dz, preferred_element_type=jnp.float32) * factor
    part_down = jnp.dot(cross_input.T, dlow, preferred_element_type=jnp.float32) * factor
    owner_up, owner_down = (
        lax.psum_scatter(part_up, "tbl", scatter_dimension=0, tiled=True),
        lax.psum_scatter(part_down, "tbl", scatter_dimension=1, tiled=True),
    )
    grad_up, grad_down = (
        lax.psum_scatter(owner_up, "grp", scatter_dimension=1, tiled=True),
        lax.psum_scatter(owner_down, "grp", scatter_dimension=0, tiled=True),
    )
    return (next_embedded, grad_up, grad_down)


def solution(mesh):
    return jax.shard_map(
        on_device,
        mesh=mesh,
        in_specs=(
            P(("grp", "tbl"), None),
            P(("grp", "tbl"), None),
            P(),
            P("tbl", None, None),
            P(("grp", "tbl"), None),
            P(("grp", "tbl"), None),
            P(),
            P(),
        ),
        out_specs=(P(("grp", "tbl"), None), P("tbl", "grp"), P("grp", "tbl")),
        check_vma=False,
    )
```

profile of v0, /device:TPU:0, one launch (start us, length us, event | category | flops | bytes accessed | tf_op | source)
XLA Modules:
  0.0 268.0 jit_solution(345015347760096953)
XLA Ops:
  7.2 1.4 copy-done
  8.6 5.0 %convolution_multiply_fusion.1 = f32[256,3456]{1,0:T(8,128)} fusion(bf16[128,3456]{1,0:T(8,128)(2,1)} %param.14, bf16[3456,256]{1,0:T(8,128)(2,1)S(1)} %copy-done, bf16[128,3456]{1,0:T(8,128)(2,1)} %param.15), kind=kOutput, calls=%fused_computation.14 | convolution fusion | flops 455671808 | bytes 7077888 | tf_op jit(solution)/shard_map/dot_general | solution.py:56
  13.7 1.1 copy-done.1
  14.8 0.3 copy-done.2
  15.1 5.4 %fusion = f32[3456,256]{0,1:T(8,128)} fusion(bf16[128,3456]{1,0:T(8,128)(2,1)S(1)} %copy-done.1, bf16[256,3456]{1,0:T(8,128)(2,1)} %param.16, bf16[128,3456]{1,0:T(8,128)(2,1)S(1)} %copy-done.2), kind=kOutput, calls=%fused_computation.15 | convolution fusion | flops 455671808 | bytes 7077888 | tf_op jit(solution)/shard_map/dot_general | solution.py:57
  20.6 36.4 %reduce-scatter.9.cloned.1.call-done = f32[64,3456]{1,0:T(8,128)} async-done(((f32[256,3456]{1,0:T(8,128)}), f32[64,3456]{1,0:T(8,128)}) %reduce-scatter.9.cloned.1.call-update) | async-done | bytes 884752 | tf_op jit(solution)/shard_map/reduce_scatter | solution.py:59
  56.9 2.9 %copy.70 = f32[64,3456]{0,1:T(8,128)} copy(f32[64,3456]{1,0:T(8,128)} %reduce-scatter.9.cloned.1.call-done) | data formatting | bytes 1769472
  60.0 0.2 multiply_reduce_fusion
  60.3 0.7 reshape.149
  60.9 3.3 %all-to-all-start = ((s32[4,1,896]{2,1,0:T(1,128)}), s32[4,1,896]{2,1,0:T(1,128)S(1)}, u32[]{:S(2)}, u32[]{:S(2)}) async-start(s32[4,1,896]{2,1,0:T(1,128)} %reshape.149), calls=%async_computation | async-start | bytes 28672 | tf_op jit(solution)/shard_map/all_to_all | solution.py:44
  64.5 0.9 reshape.151
  65.4 2.7 all-to-all-done
  68.0 3.3 %all-to-all-start.1 = ((s32[4,1,7168]{2,1,0:T(1,128)}), s32[4,1,7168]{2,1,0:T(1,128)S(1)}, u32[]{:S(2)}, u32[]{:S(2)}) async-start(s32[4,1,7168]{2,1,0:T(1,128)} %reshape.151), calls=%async_computation.1 | async-start | bytes 229376 | tf_op jit(solution)/shard_map/all_to_all | solution.py:43
  71.4 0.5 broadcast.113
  71.9 0.7 reduce.4
  72.9 2.9 %all-to-all-done.1 = s32[4,1,7168]{2,1,0:T(1,128)S(1)} async-done(((s32[4,1,7168]{2,1,0:T(1,128)}), s32[4,1,7168]{2,1,0:T(1,128)S(1)}, u32[]{:S(2)}, u32[]{:S(2)}) %all-to-all-start.1) | async-done | bytes 114720 | tf_op jit(solution)/shard_map/all_to_all | solution.py:43
  75.7 0.9 reduce.5
  76.7 0.2 reshape.152
  77.0 0.2 all_to_all.44
  77.2 22.8 %reduce-scatter.11.cloned.1.call-done = f32[3456,64]{0,1:T(8,128)} async-done(((f32[3456,256]{0,1:T(8,128)}), f32[3456,64]{0,1:T(8,128)}) %reduce-scatter.11.cloned.1.call-update) | async-done | bytes 884752 | tf_op jit(solution)/shard_map/reduce_scatter | solution.py:60
  99.9 3.0 %copy.72 = f32[3456,64]{1,0:T(8,128)} copy(f32[3456,64]{0,1:T(8,128)} %reduce-scatter.11.cloned.1.call-done) | data formatting | bytes 1769472
  102.9 127.0 %while.12 = (s32[]{:T(128)}, bf16[2,256,896]{1,2,0:T(8,128)(2,1)}, s32[2,256,7]{2,1,0:T(8,128)S(1)}, s32[2,256,56]{1,2,0:T(8,128)S(1)}, bf16[43008,128]{1,0:T(8,128)(2,1)}, /*index=5*/s32[]{:T(128)}) while((s32[]{:T(128)}, bf16[2,256,896]{1,2,0:T(8,128)(2,1)}, s32[2,256,7]{2,1,0:T(8,128)S(1)}, s32[2,256,56]{1,2,0:T(8,128)S(1)}, ...), condition=%wide.region_3.4_spmd, body=%wide.region_1.3_spmd.sunk | while | flops 5462025 | bytes 14272161 | solution.py:45
  103.4 0.4 add.114
  103.9 54.2 %gather_fusion = bf16[14336,128]{1,0:T(8,128)(2,1)} fusion(bf16[43008,128]{1,0:T(8,128)(2,1)} %get-tuple-element.159, s32[14336]{0:T(1024)S(1)} %broadcast_clamp_fusion.2), kind=kCustom, calls=%fused_computation.clone.1 | custom fusion | bytes 7397376 | tf_op jit(solution)/shard_map/while/body/eval_jaxpr/jit(_take)/gather | solution.py:15
  158.1 0.5 copy.81
  158.6 0.3 iota_compare_fusion.3
  158.9 6.3 %select_reduce_fusion.2 = bf16[256,7,128]{2,1,0:T(8,128)(2,1)S(1)} fusion(bf16[256,7,8,128]{3,2,1,0:T(8,128)(2,1)} %bitcast.58, pred[256,7,8]{2,1,0:T(8,128)(4,1)S(1)} %copy.81, pred[256,7,8]{2,1,0:T(8,128)(4,1)S(1)} %iota_compare_fusion.3), kind=kLoop, calls=%fused_computation.2.clone.1 | loop fusion | flops 5275648 | bytes 4157440 | tf_op jit(solution)/shard_map/while/body/eval_jaxpr/reduce_sum | solution.py:20
  165.2 0.3 copy.82
  165.6 0.8 constant_dynamic-update-slice_fusion.2
  166.9 0.4 add.114
  167.4 54.2 %gather_fusion = bf16[14336,128]{1,0:T(8,128)(2,1)} fusion(bf16[43008,128]{1,0:T(8,128)(2,1)} %get-tuple-element.159, s32[14336]{0:T(1024)S(1)} %broadcast_clamp_fusion.2), kind=kCustom, calls=%fused_computation.clone.1 | custom fusion | bytes 7397376 | tf_op jit(solution)/shard_map/while/body/eval_jaxpr/jit(_take)/gather | solution.py:15
  221.6 0.5 copy.81
  222.1 0.3 iota_compare_fusion.3
  222.4 6.3 %select_reduce_fusion.2 = bf16[256,7,128]{2,1,0:T(8,128)(2,1)S(1)} fusion(bf16[256,7,8,128]{3,2,1,0:T(8,128)(2,1)} %bitcast.58, pred[256,7,8]{2,1,0:T(8,128)(4,1)S(1)} %copy.81, pred[256,7,8]{2,1,0:T(8,128)(4,1)S(1)} %iota_compare_fusion.3), kind=kLoop, calls=%fused_computation.2.clone.1 | loop fusion | flops 5275648 | bytes 4157440 | tf_op jit(solution)/shard_map/while/body/eval_jaxpr/reduce_sum | solution.py:20
  228.7 0.3 copy.82
  229.1 0.8 constant_dynamic-update-slice_fusion.2
  229.9 3.7 %copy.61 = bf16[2,256,896]{2,0,1:T(2,128)(2,1)} copy(bf16[2,256,896]{1,2,0:T(8,128)(2,1)} %get-tuple-element.68) | data formatting | bytes 1835008 | tf_op jit(solution)/shard_map/while | solution.py:45
  233.5 3.7 %all-to-all-start.2 = ((bf16[2,256,896]{2,0,1:T(2,128)(2,1)}), bf16[2,256,896]{2,0,1:T(2,128)(2,1)S(1)}, u32[]{:S(2)}, u32[]{:S(2)}) async-start(bf16[2,256,896]{2,0,1:T(2,128)(2,1)} %copy.61), calls=%async_computation.2 | async-start | bytes 1835008 | tf_op jit(solution)/shard_map/all_to_all | solution.py:48
  237.3 12.7 %all-to-all-done.2 = bf16[2,256,896]{2,0,1:T(2,128)(2,1)S(1)} async-done(((bf16[2,256,896]{2,0,1:T(2,128)(2,1)}), bf16[2,256,896]{2,0,1:T(2,128)(2,1)S(1)}, u32[]{:S(2)}, u32[]{:S(2)}) %all-to-all-start.2) | async-done | bytes 917536 | tf_op jit(solution)/shard_map/all_to_all | solution.py:48
  250.1 0.7 copy.63
  250.8 1.3 reshape.127
  252.2 1.6 copy.64
  253.8 0.7 gather_fusion.1
  254.5 0.6 copy.65
  255.1 1.7 bitcast_select_fusion
  256.8 1.3 copy.66
  258.1 1.7 copy.71
  259.8 1.7 copy.73
  (48 shorter events, 2.4 us)
Async XLA Ops:
  7.2 1.5 copy-start
  7.2 49.8 %reduce-scatter.9.cloned.1.call-start = ((), (), s32[]{:S(2)}) async-start(), calls=%async_computation.7 | async-start | bytes 4423680 | tf_op jit(solution)/shard_map/reduce_scatter | solution.py:59
  13.7 1.2 copy-start.1
  13.7 1.4 copy-start.2
  13.7 86.2 %reduce-scatter.11.cloned.1.call-start = ((), (), s32[]{:S(2)}) async-start(), calls=%async_computation.8 | async-start | bytes 4423680 | tf_op jit(solution)/shard_map/reduce_scatter | solution.py:60
  20.5 39.4 %copy-start.5 = (s32[26]{0:T(128)S(1)}, s32[26]{0:T(128)}, u32[]{:S(2)}) copy-start(s32[26]{0:T(128)} %param.12) | copy-start | bytes 316
  20.5 39.5 %copy-start.4 = (s32[128,26]{0,1:T(8,128)S(1)}, s32[128,26]{0,1:T(8,128)}, u32[]{:S(2)}) copy-start(s32[128,26]{0,1:T(8,128)} %param.11) | copy-start | bytes 39940
  20.5 43.7 %copy-start.3 = (s32[128,224]{0,1:T(8,128)S(1)}, s32[128,224]{0,1:T(8,128)}, u32[]{:S(2)}) copy-start(s32[128,224]{0,1:T(8,128)} %param.10) | copy-start | bytes 344068
  20.5 237.6 %reduce-scatter.13.cloned.1.call-start = ((), (), s32[]{:S(2)}) async-start(), calls=%async_computation.9 | async-start | bytes 1990656
  60.9 7.1 %all-to-all-start = ((s32[4,1,896]{2,1,0:T(1,128)}), s32[4,1,896]{2,1,0:T(1,128)S(1)}, u32[]{:S(2)}, u32[]{:S(2)}) async-start(s32[4,1,896]{2,1,0:T(1,128)} %reshape.149), calls=%async_computation | async-start | bytes 28672 | tf_op jit(solution)/shard_map/all_to_all | solution.py:44
  68.0 7.7 %all-to-all-start.1 = ((s32[4,1,7168]{2,1,0:T(1,128)}), s32[4,1,7168]{2,1,0:T(1,128)S(1)}, u32[]{:S(2)}, u32[]{:S(2)}) async-start(s32[4,1,7168]{2,1,0:T(1,128)} %reshape.151), calls=%async_computation.1 | async-start | bytes 229376 | tf_op jit(solution)/shard_map/all_to_all | solution.py:43
  71.3 188.5 %reduce-scatter.15.cloned.1.call-start = ((), (), s32[]{:S(2)}) async-start(), calls=%async_computation.10 | async-start | bytes 1990656
  233.5 16.5 %all-to-all-start.2 = ((bf16[2,256,896]{2,0,1:T(2,128)(2,1)}), bf16[2,256,896]{2,0,1:T(2,128)(2,1)S(1)}, u32[]{:S(2)}, u32[]{:S(2)}) async-start(bf16[2,256,896]{2,0,1:T(2,128)(2,1)} %copy.61), calls=%async_computation.2 | async-start | bytes 1835008 | tf_op jit(solution)/shard_map/all_to_all | solution.py:48
Sparse Core Ops, SparseCore 0:
  13.8 43.0 reduce-scatter.8
  59.5 40.3 reduce-scatter.10
  103.4 66.5 reduce-scatter.12
  173.3 65.4 reduce-scatter.14
where the time goes:
time: 269 us; the launch traced here: 268 us
  local copies, waits for them, and re-layouts  138 us (51%)
  waiting for transfers between devices  77.4 us (29%)
  other arithmetic  17.2 us (6%)
  between operations  14 us (5%)
  starting transfers between devices  10.4 us (4%)
  matrix products  10.4 us (4%)
    gather x2, local copies, waits for them, and re-layouts, pool_rows(): jnp.take(table_flat, (ids_three + offset).reshape(-1), axis=0)  108 us
    reduce_scatter x1, waiting for transfers between devices, on_device(): lax.psum_scatter(part_up, 'tbl', scatter_dimension=0, tiled=True)  36.4 us
    reduce_scatter x1, waiting for transfers between devices, on_device(): lax.psum_scatter(part_down, 'tbl', scatter_dimension=1, tiled=True)  22.8 us
    unnamed x22, local copies, waits for them, and re-layouts  15.3 us
    all_to_all x1, waiting for transfers between devices, on_device(): lax.all_to_all(pooled, 'tbl', split_axis=1, concat_axis=2, tiled=True)  12.7 us
    reduce_sum x2, other arithmetic, pool_rows(): pooled = jnp.sum(masked, axis=2, dtype=jnp.float32)  12.6 us
    dot_general x1, matrix products, on_device(): jnp.dot(cross_input.T, dlow, preferred_element_type=jnp.float32) * factor  5.39 us
  transfers between devices with their start and end apart: 7, of which 5 were waited for; matrix products, arithmetic and copies ran while one was open for 58% of the time, Pallas kernels for 0%

commit v1 on v0

v1 whole, which is shorter than its diff:
```python
import functools
import math

import jax
import jax.numpy as jnp
from jax import lax
from jax.experimental import pallas as pl
from jax.experimental.pallas import tpu as pltpu
from jax.sharding import PartitionSpec as P

LANES = 128


def pool_kernel(maxlen, idx_ref, tab_ref, out_ref, stage, wide, acc, sem):
    owners, batch, _ = out_ref.shape
    slots, rows, width = tab_ref.shape
    per_line = LANES // maxlen
    lines = batch // per_line
    chunk = 256

    def fetch(s):
        return pltpu.make_async_copy(tab_ref.at[s], stage.at[s % 2], sem.at[s % 2])

    fetch(0).start()
    wide[pl.ds(rows, 8), :] = jnp.zeros((8, width), jnp.float32)
    for s in range(slots):
        if s + 1 < slots:
            fetch(s + 1).start()
        fetch(s).wait()

        @pl.loop(0, rows // chunk)
        def _(c):
            at = pl.ds(pl.multiple_of(c * chunk, chunk), chunk)
            wide[at, :] = stage[s % 2, at, :].astype(jnp.float32)

        @pl.loop(0, owners * lines)
        def _(g):
            src = g // lines
            line = s * lines + g % lines
            for u in range(per_line):
                got = [
                    wide[pl.ds(idx_ref[src, line, u * maxlen + k], 1), :] for k in range(maxlen)
                ]
                while len(got) > 1:
                    got = [a + b for a, b in zip(got[::2], got[1::2])] + (
                        [got[-1]] if len(got) % 2 else []
                    )
                acc[pl.ds(g * per_line + u, 1), :] = got[0]

        for o in range(owners):
            out_ref[o, :, s * width : (s + 1) * width] = acc[
                o * batch : (o + 1) * batch, :
            ].astype(jnp.bfloat16)


def pool(idx, tables, batch, maxlen):
    slots, rows, width = tables.shape
    owners = idx.shape[0]
    return pl.pallas_call(
        functools.partial(pool_kernel, maxlen),
        out_shape=jax.ShapeDtypeStruct((owners, batch, slots * width), jnp.bfloat16),
        in_specs=[
            pl.BlockSpec(memory_space=pltpu.SMEM),
            pl.BlockSpec(memory_space=pl.ANY),
        ],
        out_specs=pl.BlockSpec(memory_space=pltpu.VMEM),
        scratch_shapes=[
            pltpu.VMEM((2, rows, width), jnp.bfloat16),
            pltpu.VMEM((rows + 8, width), jnp.float32),
            pltpu.VMEM((owners * batch, width), jnp.float32),
            pltpu.SemaphoreType.DMA((2,)),
        ],
        compiler_params=pltpu.CompilerParams(vmem_limit_bytes=60 << 20),
        cost_estimate=pl.CostEstimate(
            flops=100_000_000, bytes_accessed=tables.size * 2, transcendentals=0
        ),
        name="pool",
    )(idx, tables)


def order_kernel(slot_ref, got_ref, out_ref):
    owners, batch, wide = got_ref.shape
    feats = slot_ref.shape[0]
    width = out_ref.shape[1] // feats
    slots = wide // width
    for f in range(feats):
        s = slot_ref[f]
        at = pl.ds(pl.multiple_of(lax.rem(s, slots) * width, width), width)
        out_ref[:, f * width : (f + 1) * width] = got_ref[lax.div(s, slots), :, at]


def order(slot_of_table, got, width):
    return pl.pallas_call(
        order_kernel,
        out_shape=jax.ShapeDtypeStruct(
            (got.shape[1], slot_of_table.shape[0] * width), jnp.bfloat16
        ),
        in_specs=[
            pl.BlockSpec(memory_space=pltpu.SMEM),
            pl.BlockSpec(memory_space=pltpu.VMEM),
        ],
        out_specs=pl.BlockSpec(memory_space=pltpu.VMEM),
        name="order",
    )(slot_of_table, got)


def bag_rows(next_ids, next_lengths, slot_of_table, slots, owners, rows):
    batch = next_ids.shape[0]
    slots_all = slots * owners
    maxlen = next_ids.shape[1] // slots_all
    hit = (slot_of_table[:, None] == lax.broadcasted_iota(jnp.int32, (1, slots_all), 1)).astype(
        jnp.int32
    )
    slot_lengths = jnp.sum(next_lengths[:, :, None] * hit[None, :, :], axis=1)
    keep = lax.broadcasted_iota(jnp.int32, (batch, slots_all, maxlen), 2) < slot_lengths[:, :, None]
    idx = jnp.where(keep, next_ids.reshape(batch, slots_all, maxlen), rows)
    return idx.transpose(1, 0, 2).reshape(owners, slots * batch * maxlen // LANES, LANES)


def on_device(
    next_ids, next_lengths, slot_of_table, tables, cross_input, cotangent, up_weight, down_weight
):
    batch = next_ids.shape[0]
    owners = lax.axis_size("tbl")
    slots, rows, width = tables.shape
    maxlen = next_ids.shape[1] // (slots * owners)
    idx = bag_rows(next_ids, next_lengths, slot_of_table, slots, owners, rows)
    low = jnp.dot(cross_input, down_weight, preferred_element_type=jnp.float32).astype(jnp.bfloat16)
    dz = (cotangent.astype(jnp.float32) * cross_input.astype(jnp.float32)).astype(jnp.bfloat16)
    dlow = jnp.dot(dz, up_weight.T, preferred_element_type=jnp.float32).astype(jnp.bfloat16)
    total = batch * lax.axis_size("grp") * owners
    factor = 1.0 / math.sqrt(total)
    part_up = jnp.dot(low.T, dz, preferred_element_type=jnp.float32) * factor
    part_down = jnp.dot(cross_input.T, dlow, preferred_element_type=jnp.float32) * factor
    part_up, part_down = part_up.astype(jnp.bfloat16), part_down.astype(jnp.bfloat16)
    owner_up, owner_down = (
        lax.psum_scatter(part_up, "tbl", scatter_dimension=0, tiled=True).astype(jnp.float32),
        lax.psum_scatter(part_down, "tbl", scatter_dimension=1, tiled=True).astype(jnp.float32),
    )
    got_idx = lax.all_to_all(idx, "tbl", split_axis=0, concat_axis=0, tiled=True)
    pooled = pool(got_idx, tables, batch, maxlen)
    returned = lax.all_to_all(pooled, "tbl", split_axis=0, concat_axis=0, tiled=True)
    next_embedded = order(slot_of_table, returned, width)
    grad_up, grad_down = (
        lax.psum_scatter(owner_up, "grp", scatter_dimension=1, tiled=True),
        lax.psum_scatter(owner_down, "grp", scatter_dimension=0, tiled=True),
    )
    return (next_embedded, grad_up, grad_down)


def solution(mesh):
    return jax.shard_map(
        on_device,
        mesh=mesh,
        in_specs=(
            P(("grp", "tbl"), None),
            P(("grp", "tbl"), None),
            P(),
            P("tbl", None, None),
            P(("grp", "tbl"), None),
            P(("grp", "tbl"), None),
            P(),
            P(),
        ),
        out_specs=(P(("grp", "tbl"), None), P("tbl", "grp"), P("grp", "tbl")),
        check_vma=False,
    )
```

time: 269 us -> 225 us (0.84)
  local copies, waits for them, and re-layouts: 138 us -> 15.4 us
  waiting for transfers between devices: 77.4 us -> 123 us
  Pallas kernels: 0 us -> 35.3 us
  blocking collectives: 0 us -> 24.8 us
  other arithmetic: 17.2 us -> 3.03 us
  starting transfers between devices: 10.4 us -> 0.16 us
    gather x4 -> x0, local copies, waits for them, and re-layouts: 110 us -> none  [the longest x2 108 us: pool_rows(): jnp.take(table_flat, (ids_three + offset).reshape(-1), axis=0)]
    unnamed x6, waiting for transfers between devices: 0.07 us -> 67.7 us
    pallas_call x0 -> x2, Pallas kernels: none -> 35.3 us  [the longest x1 33 us: pool(): pl.pallas_call(functools.partial(pool_kernel, maxlen), out_shape=jax.Shap...]
    all_to_all x0 -> x2, blocking collectives: none -> 24.8 us  [the longest x1 17.3 us: on_device(): lax.all_to_all(pooled, 'tbl', split_axis=0, concat_axis=0, tiled=True)]
    all_to_all x3 -> x0, waiting for transfers between devices: 18.2 us -> none  [the longest x1 12.7 us: on_device(): lax.all_to_all(pooled, 'tbl', split_axis=1, concat_axis=2, tiled=True)]
    reduce_sum x3 -> x1, other arithmetic: 12.8 us -> 0.18 us  [bag_rows(): slot_lengths = jnp.sum(next_lengths[:, :, None] * hit[None, :, :], axis=1)]
    reduce_scatter x1, waiting for transfers between devices: 36.4 us -> 25.7 us  [on_device(): lax.psum_scatter(part_up, 'tbl', scatter_dimension=0, tiled=True)]
    all_to_all x3 -> x0, starting transfers between devices: 10.3 us -> none  [the longest x1 3.68 us: on_device(): lax.all_to_all(pooled, 'tbl', split_axis=1, concat_axis=2, tiled=True)]
  transfers between devices with their start and end apart: 7 -> 4, of which waited for: 5 -> 4; matrix products, arithmetic and copies ran while one was open for 58% -> 8% of each run, Pallas kernels for 0% -> 16%
where the time goes in v1:
time: 225 us; the launch traced here: 224 us
  waiting for transfers between devices  123 us (55%)
  Pallas kernels  35.3 us (16%)
  blocking collectives  24.8 us (11%)
  local copies, waits for them, and re-layouts  15.4 us (7%)
  between operations  13.8 us (6%)
  matrix products  9.29 us (4%)
  other arithmetic  3.03 us (1%)
    unnamed x6, waiting for transfers between devices  67.7 us
    pallas_call x1, Pallas kernels, pool(): pl.pallas_call(functools.partial(pool_kernel, maxlen), out_shape=jax.Shap...  33 us
    reduce_scatter x1, waiting for transfers between devices, on_device(): lax.psum_scatter(part_down, 'tbl', scatter_dimension=1, tiled=True)  29.2 us
    reduce_scatter x1, waiting for transfers between devices, on_device(): lax.psum_scatter(part_up, 'tbl', scatter_dimension=0, tiled=True)  25.7 us
    all_to_all x1, blocking collectives, on_device(): lax.all_to_all(pooled, 'tbl', split_axis=0, concat_axis=0, tiled=True)  17.3 us
    unnamed x16, local copies, waits for them, and re-layouts  11.3 us
    all_to_all x1, blocking collectives, on_device(): lax.all_to_all(idx, 'tbl', split_axis=0, concat_axis=0, tiled=True)  7.46 us
    dot_general x1, matrix products, on_device(): jnp.dot(cross_input.T, dlow, preferred_element_type=jnp.float32) * factor  4.86 us
  transfers between devices with their start and end apart: 4, of which 4 were waited for; matrix products, arithmetic and copies ran while one was open for 8% of the time, Pallas kernels for 16%

profile of v1, /device:TPU:0, one launch (start us, length us, event | category | flops | bytes accessed | tf_op | source)
XLA Modules:
  0.0 224.4 jit_solution(12670796000744787463)
XLA Ops:
  7.2 0.0 copy-start
  7.2 0.0 reduce-scatter.9.cloned.1.call-start
  7.2 1.4 copy-done
  8.6 4.4 %fusion = bf16[256,3456]{1,0:T(8,128)(2,1)} fusion(bf16[128,3456]{1,0:T(8,128)(2,1)} %param.12, bf16[3456,256]{1,0:T(8,128)(2,1)S(1)} %copy-done, bf16[128,3456]{1,0:T(8,128)(2,1)} %param.13), kind=kOutput, calls=%fused_computation.2 | convolution fusion | flops 456556544 | bytes 5308416 | tf_op jit(solution)/shard_map/dot_general | solution.py:133
  13.1 0.0 copy-start.1
  13.1 0.0 copy-start.2
  13.1 0.0 reduce-scatter.9.cloned.1.call-update
  13.1 0.0 reduce-scatter.11.cloned.1.call-start
  13.2 1.1 copy-done.1
  14.2 0.3 copy-done.2
  14.5 4.9 %fusion.2 = bf16[3456,256]{0,1:T(8,128)(2,1)} fusion(bf16[128,3456]{1,0:T(8,128)(2,1)S(1)} %copy-done.1, bf16[256,3456]{1,0:T(8,128)(2,1)} %param.14, bf16[128,3456]{1,0:T(8,128)(2,1)S(1)} %copy-done.2), kind=kOutput, calls=%fused_computation.4 | convolution fusion | flops 456556544 | bytes 5308416 | tf_op jit(solution)/shard_map/dot_general | solution.py:134
  19.4 0.0 reduce-scatter.11.cloned.1.call-update
  19.4 0.0 reduce-scatter.13.cloned.1.call-start
  19.4 25.7 %reduce-scatter.9.cloned.1.call-done = bf16[64,3456]{1,0:T(8,128)(2,1)} async-done(((bf16[256,3456]{1,0:T(8,128)(2,1)}), bf16[64,3456]{1,0:T(8,128)(2,1)}) %reduce-scatter.9.cloned.1.call-update) | async-done | bytes 442384 | tf_op jit(solution)/shard_map/reduce_scatter | solution.py:137
  45.2 2.6 %copy.18 = f32[64,3456]{0,1:T(8,128)} copy(bf16[64,3456]{1,0:T(8,128)(2,1)} %reduce-scatter.9.cloned.1.call-done) | data formatting | bytes 1327104
  47.7 0.0 reduce-scatter.13.cloned.1.call-update
  47.7 0.0 copy-start.3
  47.8 0.0 reduce-scatter.15.cloned.1.call-start
  47.8 29.2 %reduce-scatter.11.cloned.1.call-done = bf16[3456,64]{0,1:T(8,128)(2,1)} async-done(((bf16[3456,256]{0,1:T(8,128)(2,1)}), bf16[3456,64]{0,1:T(8,128)(2,1)}) %reduce-scatter.11.cloned.1.call-update) | async-done | bytes 442384 | tf_op jit(solution)/shard_map/reduce_scatter | solution.py:138
  77.0 2.5 %copy.20 = f32[3456,64]{1,0:T(8,128)} copy(bf16[3456,64]{0,1:T(8,128)(2,1)} %reduce-scatter.11.cloned.1.call-done) | data formatting | bytes 1327104
  79.5 0.0 copy-start.5
  79.5 0.0 copy-start.4
  79.5 0.0 reduce-scatter.15.cloned.1.call-update
  79.5 0.0 copy-done.3
  79.5 1.8 copy.17
  81.3 0.0 copy-done.5
  81.3 0.1 fusion.3
  81.4 0.0 copy-done.4
  81.4 0.2 multiply_reduce_fusion
  81.6 2.8 %select_bitcast_fusion = s32[28,128,8]{2,1,0:T(8,128)} fusion(s32[128,28,8]{2,0,1:T(8,128)} %copy.17, s32[128,28]{0,1:T(8,128)S(1)} %multiply_reduce_fusion), kind=kLoop, calls=%fused_computation.5 | loop fusion | flops 57344 | bytes 243712 | tf_op jit(solution)/shard_map/transpose | solution.py:117
  84.4 2.3 %reshape.34 = s32[4,56,128]{2,1,0:T(8,128)S(1)} reshape(s32[28,128,8]{2,1,0:T(8,128)} %select_bitcast_fusion) | data formatting | bytes 229376 | tf_op jit(solution)/shard_map/reshape | solution.py:117
  86.7 7.5 %all_to_all.10.idx_ref = s32[4,56,128]{2,1,0:T(8,128)} all-to-all(s32[4,56,128]{2,1,0:T(8,128)S(1)} %reshape.34), channel_id=1, replica_groups=mesh['grp'=8,'tbl'=4] {'tbl'}, dimensions={0} | all-to-all | bytes 229376 | tf_op jit(solution)/shard_map/all_to_all | solution.py:140
  94.1 33.0 %pool.1 = bf16[4,128,896]{2,1,0:T(8,128)(2,1)} custom-call(s32[4,56,128]{2,1,0:T(8,128)} %all_to_all.10.idx_ref, bf16[7,6144,128]{2,1,0:T(8,128)(2,1)} %tab_ref.1), custom_call_target="tpu_custom_call" | custom-call | flops 100000000 | bytes 11010048 | tf_op jit(solution)/shard_map/pool/pallas_call | solution.py:59
  127.2 17.3 %all_to_all.11.got_ref = bf16[4,128,896]{2,1,0:T(8,128)(2,1)} all-to-all(bf16[4,128,896]{2,1,0:T(8,128)(2,1)} %pool.1), channel_id=1, replica_groups=mesh['grp'=8,'tbl'=4] {'tbl'}, dimensions={0} | all-to-all | bytes 1835008 | tf_op jit(solution)/shard_map/all_to_all | solution.py:142
  144.5 2.3 %order.1 = bf16[128,3328]{1,0:T(8,128)(2,1)} custom-call(s32[26]{0:T(128)} %slot_ref.1, bf16[4,128,896]{2,1,0:T(8,128)(2,1)} %all_to_all.11.got_ref), custom_call_target="tpu_custom_call" | custom-call | tf_op jit(solution)/shard_map/order/pallas_call | solution.py:93
  146.8 0.2 reduce-scatter.13.cloned.1.call-done
  147.1 1.7 copy.19
  148.8 67.4 %reduce-scatter.15.cloned.1.call-done = f32[432,64]{1,0:T(8,128)} async-done(((f32[3456,64]{1,0:T(8,128)}), f32[432,64]{1,0:T(8,128)}) %reduce-scatter.15.cloned.1.call-update) | async-done | bytes 110608
  216.1 1.7 copy.21
Async XLA Ops:
  7.2 1.5 copy-start
  7.2 38.0 %reduce-scatter.9.cloned.1.call-start = ((), (), s32[]{:S(2)}) async-start(), calls=%async_computation.6 | async-start | bytes 2211840 | tf_op jit(solution)/shard_map/reduce_scatter | solution.py:137
  13.1 1.2 copy-start.1
  13.1 1.4 copy-start.2
  13.1 63.9 %reduce-scatter.11.cloned.1.call-start = ((), (), s32[]{:S(2)}) async-start(), calls=%async_computation.7 | async-start | bytes 2211840 | tf_op jit(solution)/shard_map/reduce_scatter | solution.py:138
  19.4 127.7 %reduce-scatter.13.cloned.1.call-start = ((), (), s32[]{:S(2)}) async-start(), calls=%async_computation.8 | async-start | bytes 1990656
  47.7 31.8 %copy-start.3 = (s32[128,224]{0,1:T(8,128)S(1)}, s32[128,224]{0,1:T(8,128)}, u32[]{:S(2)}) copy-start(s32[128,224]{0,1:T(8,128)} %param.8) | copy-start | bytes 344068
  47.8 168.4 %reduce-scatter.15.cloned.1.call-start = ((), (), s32[]{:S(2)}) async-start(), calls=%async_computation.9 | async-start | bytes 1990656
  79.5 1.8 copy-start.5
  79.5 1.9 copy-start.4
Sparse Core Ops, SparseCore 0:
  13.2 31.8 reduce-scatter.8
  47.7 29.1 reduce-scatter.10
  80.4 66.5 reduce-scatter.12
  150.4 65.6 reduce-scatter.14

commit v2 on v1

--- a/solution.py
+++ b/solution.py
@@ -117,7 +117,7 @@
     return idx.transpose(1, 0, 2).reshape(owners, slots * batch * maxlen // LANES, LANES)
 
 
-def on_device(
+def plain(
     next_ids, next_lengths, slot_of_table, tables, cross_input, cotangent, up_weight, down_weight
 ):
     batch = next_ids.shape[0]
@@ -148,6 +148,327 @@
     return (next_embedded, grad_up, grad_down)
 
 
+def step_kernel(
+    maxlen,
+    factor,
+    split,
+    checkpoints,
+    idx_ref,
+    slot_ref,
+    tab_ref,
+    x_ref,
+    ct_ref,
+    up_ref,
+    down_ref,
+    emb_ref,
+    grad_ref,
+    idx_in,
+    idx_s,
+    part,
+    c_in,
+    a_in,
+    b_in,
+    a2_in,
+    b2_in,
+    z_in,
+    stage,
+    wide,
+    acc,
+    pooled,
+    got,
+    tab_sem,
+    smem_sem,
+    idx_sem,
+    core_sem,
+    one_sem,
+    two_sem,
+    z_sem,
+    pool_sem,
+):
+    owners, zs, _, high, lanes = part.shape
+    slots, rows, width = tab_ref.shape
+    batch = x_ref.shape[0]
+    rank = down_ref.shape[1]
+    cols = rank // owners
+    per_line = LANES // maxlen
+    lines = batch // per_line
+    chunk = 256
+    g, t = lax.axis_index("grp"), lax.axis_index("tbl")
+    z, x = g // 2, g % 2
+    core = t + 1 - 2 * (t % 2)
+    far = (t + 2) % owners
+    other = 1 - x
+    side = g + 1 - 2 * x
+
+    def fetch(s):
+        return pltpu.make_async_copy(tab_ref.at[s], stage.at[s % 2], tab_sem.at[s % 2])
+
+    def send(src, dst, sems, n, device):
+        return pltpu.make_async_remote_copy(
+            src_ref=src,
+            dst_ref=dst,
+            send_sem=sems.at[0, n],
+            recv_sem=sems.at[1, n],
+            device_id=device,
+            device_id_type=pl.DeviceIdType.MESH,
+        )
+
+    fetch(0).start()
+    barrier = pltpu.get_barrier_semaphore()
+    near = [(g, (t + d) % owners) for d in range(1, owners)] + [(side, t)]
+    near += [((z + d) % zs * 2 + x, t) for d in range(1, zs)]
+    for device in near:
+        pl.semaphore_signal(
+            barrier, inc=1, device_id=device, device_id_type=pl.DeviceIdType.MESH
+        )
+    pl.semaphore_wait(barrier, len(near))
+
+    ids_out = [
+        send(idx_ref.at[(t + d) % owners], idx_in.at[t], idx_sem, d - 1, (g, (t + d) % owners))
+        for d in range(1, owners)
+    ]
+    for copy in ids_out:
+        copy.start()
+    keep_ids = pltpu.make_async_copy(idx_ref.at[t], idx_s.at[t], smem_sem.at[0])
+    keep_ids.start()
+
+    low = jnp.dot(x_ref[...], down_ref[...], preferred_element_type=jnp.float32).astype(jnp.bfloat16)
+    dz = (ct_ref[...].astype(jnp.float32) * x_ref[...].astype(jnp.float32)).astype(jnp.bfloat16)
+    ct = dz
+    dlow = lax.dot_general(
+        dz, up_ref[...], (((1,), (1,)), ((), ())), preferred_element_type=jnp.float32
+    ).astype(jnp.bfloat16)
+    first = (((0,), (0,)), ((), ()))
+    for block in range(2 * zs):
+        begin = block * high
+        edge = begin // LANES * LANES
+        stop = -(-(begin + high) // LANES) * LANES
+        up = lax.dot_general(ct[:, edge:stop], low, first, preferred_element_type=jnp.float32)
+        down = lax.dot_general(
+            x_ref[:, edge:stop], dlow, first, preferred_element_type=jnp.float32
+        )
+        up = (up[begin - edge : begin - edge + high] * factor).astype(jnp.bfloat16)
+        down = (down[begin - edge : begin - edge + high] * factor).astype(jnp.bfloat16)
+        for o in range(owners):
+            part[o, block // 2, block % 2] = jnp.concatenate(
+                [up[:, o * cols : (o + 1) * cols], down[:, o * cols : (o + 1) * cols]], axis=1
+            )
+
+    cross = [
+        send(part.at[core], c_in.at[0], core_sem, 0, (g, core)),
+        send(part.at[(core + 2) % owners], c_in.at[1], core_sem, 1, (g, core)),
+    ]
+    for copy in cross:
+        copy.start()
+
+    for copy in ids_out:
+        copy.wait()
+    keep_ids.wait()
+    got_ids = [
+        pltpu.make_async_copy(
+            idx_in.at[(t + d) % owners], idx_s.at[(t + d) % owners], smem_sem.at[d]
+        )
+        for d in range(1, owners)
+    ]
+    for copy in got_ids:
+        copy.start()
+    for copy in got_ids:
+        copy.wait()
+
+    low_rows, high_rows = pl.ds(0, split), pl.ds(split, high - split)
+
+    def add(where, value):
+        part[where] = (part[where].astype(jnp.float32) + value.astype(jnp.float32)).astype(
+            jnp.bfloat16
+        )
+
+    one = [
+        send(part.at[far, :, :, low_rows], a_in, one_sem, 0, (g, far)),
+        send(part.at[t, :, other, high_rows], b_in.at[0], one_sem, 1, (side, t)),
+        send(part.at[far, :, other, high_rows], b_in.at[1], one_sem, 2, (side, t)),
+    ]
+    two = [
+        send(part.at[t, :, other, low_rows], a2_in, two_sem, 0, (side, t)),
+        send(part.at[far, :, x, high_rows], b2_in, two_sem, 1, (g, far)),
+    ]
+    last = [
+        send(
+            part.at[t, (z + d) % zs, x], z_in.at[d - 1], z_sem, d - 1, ((z + d) % zs * 2 + x, t)
+        )
+        for d in range(1, zs)
+    ]
+
+    def after_core():
+        for copy in cross:
+            copy.wait()
+        for n, o in ((1, far), (0, t)):
+            for k in range(zs):
+                for j in range(2):
+                    add((o, k, j), c_in[n, k, j])
+        for copy in one:
+            copy.start()
+
+    def after_one():
+        for copy in one:
+            copy.wait()
+        for k in range(zs):
+            add((t, k, other, low_rows), a_in[k, other])
+            add((far, k, x, high_rows), b_in[1, k])
+        for copy in two:
+            copy.start()
+        for k in range(zs):
+            add((t, k, x, low_rows), a_in[k, x])
+            add((t, k, x, high_rows), b_in[0, k])
+
+    def after_two():
+        for copy in two:
+            copy.wait()
+        for k in range(zs):
+            add((t, k, x, low_rows), a2_in[k])
+            add((t, k, x, high_rows), b2_in[k])
+        for copy in last:
+            copy.start()
+
+    stages = [after_core, after_one, after_two]
+    returns = []
+    wide[pl.ds(rows, 8), :] = jnp.zeros((8, width), jnp.float32)
+    for s in range(slots):
+        if s + 1 < slots:
+            fetch(s + 1).start()
+        fetch(s).wait()
+
+        @pl.loop(0, rows // chunk)
+        def _(c):
+            at = pl.ds(pl.multiple_of(c * chunk, chunk), chunk)
+            wide[at, :] = stage[s % 2, at, :].astype(jnp.float32)
+
+        @pl.loop(0, owners * lines)
+        def _(i):
+            src = i // lines
+            line = s * lines + i % lines
+            for u in range(per_line):
+                held = [
+                    wide[pl.ds(idx_s[src, line, u * maxlen + k], 1), :] for k in range(maxlen)
+                ]
+                while len(held) > 1:
+                    held = [a + b for a, b in zip(held[::2], held[1::2])] + (
+                        [held[-1]] if len(held) % 2 else []
+                    )
+                acc[pl.ds(i * per_line + u, 1), :] = held[0]
+
+        for n, at in enumerate(checkpoints):
+            if at == s:
+                stages[n]()
+        got[t, s] = acc[pl.ds(pl.multiple_of(t * batch, batch), batch), :].astype(jnp.bfloat16)
+        for d in range(1, owners):
+            o = (t + d) % owners
+            pooled[d - 1, s] = acc[pl.ds(pl.multiple_of(o * batch, batch), batch), :].astype(
+                jnp.bfloat16
+            )
+            copy = send(
+                pooled.at[d - 1, s], got.at[t, s], pool_sem, s * (owners - 1) + d - 1, (g, o)
+            )
+            copy.start()
+            returns.append(copy)
+
+    for copy in last:
+        copy.wait()
+    total = part[t, z, x].astype(jnp.float32)
+    for d in range(1, zs):
+        total += z_in[d - 1].astype(jnp.float32)
+    grad_ref[...] = total
+    for copy in returns:
+        copy.wait()
+    for f in range(slot_ref.shape[0]):
+        s = slot_ref[f]
+        emb_ref[:, f * width : (f + 1) * width] = got[lax.div(s, slots), lax.rem(s, slots)]
+
+
+def fused_step(idx, slot_of_table, tables, cross_input, cotangent, up_weight, down_weight, maxlen, factor):
+    groups, owners = lax.axis_size("grp"), lax.axis_size("tbl")
+    slots, rows, width = tables.shape
+    batch, depth = cross_input.shape
+    zs, high = groups // 2, depth // groups
+    split = (high // 2 + 15) // 16 * 16
+    sems = pltpu.SemaphoreType.DMA
+    bf16 = jnp.bfloat16
+    vmem = pl.BlockSpec(memory_space=pltpu.VMEM)
+    checkpoints = (0, min(3, slots - 1), min(5, slots - 1))
+    return pl.pallas_call(
+        functools.partial(step_kernel, maxlen, factor, split, checkpoints),
+        out_shape=(
+            jax.ShapeDtypeStruct((batch, slot_of_table.shape[0] * width), bf16),
+            jax.ShapeDtypeStruct((high, LANES), jnp.float32),
+        ),
+        in_specs=[
+            vmem,
+            pl.BlockSpec(memory_space=pltpu.SMEM),
+            pl.BlockSpec(memory_space=pl.ANY),
+            vmem,
+            vmem,
+            vmem,
+            vmem,
+        ],
+        out_specs=(vmem, vmem),
+        scratch_shapes=[
+            pltpu.VMEM(idx.shape, jnp.int32),
+            pltpu.SMEM(idx.shape, jnp.int32),
+            pltpu.VMEM((owners, zs, 2, high, LANES), bf16),
+            pltpu.VMEM((2, zs, 2, high, LANES), bf16),
+            pltpu.VMEM((zs, 2, split, LANES), bf16),
+            pltpu.VMEM((2, zs, high - split, LANES), bf16),
+            pltpu.VMEM((zs, split, LANES), bf16),
+            pltpu.VMEM((zs, high - split, LANES), bf16),
+            pltpu.VMEM((max(zs - 1, 1), high, LANES), bf16),
+            pltpu.VMEM((2, rows, width), bf16),
+            pltpu.VMEM((rows + 8, width), jnp.float32),
+            pltpu.VMEM((owners * batch, width), jnp.float32),
+            pltpu.VMEM((owners - 1, slots, batch, width), bf16),
+            pltpu.VMEM((owners, slots, batch, width), bf16),
+            sems((2,)),
+            sems((owners,)),
+            sems((2, owners - 1)),
+            sems((2, 2)),
+            sems((2, 3)),
+            sems((2, 2)),
+            sems((2, max(zs - 1, 1))),
+            sems((2, slots * (owners - 1))),
+        ],
+        compiler_params=pltpu.CompilerParams(
+            collective_id=0, has_side_effects=True, vmem_limit_bytes=56 << 20
+        ),
+        name="fused_step",
+    )(idx, slot_of_table, tables, cross_input, cotangent, up_weight, down_weight)
+
+
+def on_device(
+    next_ids, next_lengths, slot_of_table, tables, cross_input, cotangent, up_weight, down_weight
+):
+    groups, owners = lax.axis_size("grp"), lax.axis_size("tbl")
+    batch, depth = cross_input.shape
+    rank = down_weight.shape[1]
+    slots, rows, _ = tables.shape
+    if owners != 4 or groups % 2 or depth % (16 * groups) or rank * 2 != owners * LANES:
+        return plain(
+            next_ids,
+            next_lengths,
+            slot_of_table,
+            tables,
+            cross_input,
+            cotangent,
+            up_weight,
+            down_weight,
+        )
+    maxlen = next_ids.shape[1] // (slots * owners)
+    factor = 1.0 / math.sqrt(batch * groups * owners)
+    idx = bag_rows(next_ids, next_lengths, slot_of_table, slots, owners, rows)
+    next_embedded, grads = fused_step(
+        idx, slot_of_table, tables, cross_input, cotangent, up_weight, down_weight, maxlen, factor
+    )
+    half = LANES // 2
+    return next_embedded, grads[:, :half].T, grads[:, half:]
+
+
 def solution(mesh):
     return jax.shard_map(
         on_device,

time: 225 us -> 62 us (0.28)
  waiting for transfers between devices: 123 us -> 0 us
  blocking collectives: 24.8 us -> 0 us
  Pallas kernels: 35.3 us -> 49.8 us
  between operations: 13.8 us -> 0.67 us
  matrix products: 9.29 us -> 0 us
  local copies, waits for them, and re-layouts: 15.4 us -> 7.87 us
    unnamed x6 -> x0, waiting for transfers between devices: 67.7 us -> none
    reduce_scatter x2 -> x0, waiting for transfers between devices: 54.9 us -> none  [the longest x1 29.2 us: on_device(): lax.psum_scatter(part_down, 'tbl', scatter_dimension=1, tiled=True)]
    all_to_all x2 -> x0, blocking collectives: 24.8 us -> none  [the longest x1 17.3 us: on_device(): lax.all_to_all(pooled, 'tbl', split_axis=0, concat_axis=0, tiled=True)]
    pallas_call x2 -> x1, Pallas kernels: 35.3 us -> 49.8 us  [fused_step(): pl.pallas_call(functools.partial(step_kernel, maxlen, factor, split, chec...]
    dot_general x2 -> x0, matrix products: 9.29 us -> none  [the longest x1 4.86 us: on_device(): jnp.dot(cross_input.T, dlow, preferred_element_type=jnp.float32) * factor]
    unnamed x16 -> x5, local copies, waits for them, and re-layouts: 11.3 us -> 2.45 us
  transfers between devices with their start and end apart: 4 -> 0, of which waited for: 4 -> 0; matrix products, arithmetic and copies ran while one was open for 8% -> 0% of each run, Pallas kernels for 16% -> 0%
where the time goes in v2:
time: 62 us; the launch traced here: 61.8 us
  Pallas kernels  49.8 us (80%)
  local copies, waits for them, and re-layouts  7.87 us (13%)
  other arithmetic  3.47 us (6%)
  between operations  0.67 us (1%)
    pallas_call x1, Pallas kernels, fused_step(): pl.pallas_call(functools.partial(step_kernel, maxlen, factor, split, chec...  49.8 us
    reshape x1, local copies, waits for them, and re-layouts, bag_rows(): idx = jnp.where(keep, next_ids.reshape(batch, slots_all, maxlen), rows)  2.71 us
    unnamed x5, local copies, waits for them, and re-layouts  2.45 us
    transpose x1, other arithmetic, bag_rows(): idx.transpose(1, 0, 2)  1.85 us
    reshape x1, local copies, waits for them, and re-layouts, bag_rows(): idx.transpose(1, 0, 2)  1.47 us

profile of v2, /device:TPU:0, one launch (start us, length us, event | category | flops | bytes accessed | tf_op | source)
XLA Modules:
  0.0 61.8 jit_solution(10644142777255620923)
XLA Ops:
  0.6 0.7 %fusion = s32[26,28]{1,0:T(8,128)S(1)} fusion(s32[26]{0:T(128)} %slot_ref.1), kind=kLoop, calls=%fused_computation.5 | loop fusion | flops 1456 | bytes 3016 | tf_op jit(solution)/shard_map/convert_element_type | solution.py:111
  1.4 0.9 %multiply_reduce_fusion = s32[128,28]{0,1:T(8,128)S(1)} fusion(s32[26,28]{1,0:T(8,128)S(1)} %fusion, s32[128,26]{0,1:T(8,128)} %param.9), kind=kLoop, calls=%fused_computation.2 | loop fusion | flops 182784 | bytes 30560 | tf_op jit(solution)/shard_map/reduce_sum | solution.py:114
  2.3 2.7 %copy.19 = s32[128,28,8]{2,0,1:T(8,128)} copy(s32[128,28,8]{0,2,1:T(8,128)} %bitcast.5) | data formatting | bytes 229376 | tf_op jit(solution)/shard_map/reshape | solution.py:116
  5.0 1.8 %select_bitcast_fusion = s32[28,128,8]{2,1,0:T(8,128)S(1)} fusion(s32[128,28,8]{2,0,1:T(8,128)} %copy.19, s32[128,28]{0,1:T(8,128)S(1)} %multiply_reduce_fusion), kind=kLoop, calls=%fused_computation | loop fusion | flops 57344 | bytes 243712 | tf_op jit(solution)/shard_map/transpose | solution.py:117
  6.8 1.5 %reshape.34.idx_ref = s32[4,56,128]{2,1,0:T(8,128)} reshape(s32[28,128,8]{2,1,0:T(8,128)S(1)} %select_bitcast_fusion) | data formatting | bytes 229376 | tf_op jit(solution)/shard_map/reshape | solution.py:117
  8.3 49.8 %fused_step.1 = (bf16[128,3328]{1,0:T(8,128)(2,1)}, f32[432,128]{1,0:T(8,128)}) custom-call(s32[4,56,128]{2,1,0:T(8,128)} %reshape.34.idx_ref, s32[26]{0:T(128)} %slot_ref.1, bf16[7,6144,128]{2,1,0:T(8,128)(2,1)} %tab_ref.1, bf16[128,3456]{1,0:T(8,128)(2,1)} %x_ref.1, bf16[128,3456]{1,0:T(8,128)(2,1)} %ct_ref.1, bf16[256,3456]{1,0:T(8,128)(2,1)} %up_ref.1, ...), custom_call_target="tpu_custom_call" | custom-call | tf_op jit(solution)/shard_map/fused_step/pallas_call | solution.py:397
  58.1 0.0 copy-start
  58.1 1.2 %fusion.1 = (f32[432,64]{1,0:T(8,128)S(1)}, f32[64,432]{0,1:T(8,128)S(1)}) fusion(f32[432,128]{1,0:T(8,128)} %get-tuple-element.6), kind=kLoop, calls=%fused_computation.6 | loop fusion | bytes 442368 | tf_op jit(solution)/shard_map/slice | solution.py:469
  59.3 0.8 %copy.21 = f32[432,64]{0,1:T(8,128)} copy(f32[432,64]{1,0:T(8,128)S(1)} %get-tuple-element.16) | data formatting | bytes 221184
  60.1 0.8 %copy.20 = f32[64,432]{1,0:T(8,128)} copy(f32[64,432]{0,1:T(8,128)S(1)} %get-tuple-element.17) | data formatting | bytes 221184
  60.9 0.0 copy-done
  60.9 0.9 %copy.23 = bf16[128,3328]{1,0:T(8,128)(2,1)} copy(bf16[128,3328]{1,0:T(8,128)(2,1)S(1)} %copy-done) | data formatting | bytes 1703936
Async XLA Ops:
  58.1 2.8 %copy-start = (bf16[128,3328]{1,0:T(8,128)(2,1)S(1)}, bf16[128,3328]{1,0:T(8,128)(2,1)}, u32[]{:S(2)}) copy-start(bf16[128,3328]{1,0:T(8,128)(2,1)} %get-tuple-element.21) | copy-start | bytes 2555908

commit v3 on v2

--- a/solution.py
+++ b/solution.py
@@ -153,15 +153,22 @@
     factor,
     split,
     checkpoints,
-    idx_ref,
+    ids_ref,
+    len_ref,
     slot_ref,
     tab_ref,
+    x_hbm,
+    ct_hbm,
+    up_hbm,
+    down_hbm,
+    emb_ref,
+    grad_up_ref,
+    grad_down_ref,
     x_ref,
     ct_ref,
     up_ref,
     down_ref,
-    emb_ref,
-    grad_ref,
+    idx_ref,
     idx_in,
     idx_s,
     part,
@@ -184,14 +191,14 @@
     two_sem,
     z_sem,
     pool_sem,
+    load_sem,
 ):
     owners, zs, _, high, lanes = part.shape
     slots, rows, width = tab_ref.shape
     batch = x_ref.shape[0]
     rank = down_ref.shape[1]
     cols = rank // owners
-    per_line = LANES // maxlen
-    lines = batch // per_line
+    group = 16
     chunk = 256
     g, t = lax.axis_index("grp"), lax.axis_index("tbl")
     z, x = g // 2, g % 2
@@ -213,6 +220,14 @@
             device_id_type=pl.DeviceIdType.MESH,
         )
 
+    loads = [
+        pltpu.make_async_copy(a, b, load_sem.at[n])
+        for n, (a, b) in enumerate(
+            ((x_hbm, x_ref), (down_hbm, down_ref), (ct_hbm, ct_ref), (up_hbm, up_ref))
+        )
+    ]
+    for copy in loads:
+        copy.start()
     fetch(0).start()
     barrier = pltpu.get_barrier_semaphore()
     near = [(g, (t + d) % owners) for d in range(1, owners)] + [(side, t)]
@@ -221,6 +236,23 @@
         pl.semaphore_signal(
             barrier, inc=1, device_id=device, device_id_type=pl.DeviceIdType.MESH
         )
+
+    feats, span = slot_ref.shape[0], ids_ref.shape[0]
+    each = slots * maxlen
+    feat = lax.broadcasted_iota(jnp.int32, (span, feats), 1)
+    entry = lax.broadcasted_iota(jnp.int32, (span, feats), 0)
+    held_by = jnp.zeros((span, feats), jnp.int32)
+    for f in range(feats):
+        held_by = jnp.where(feat == f, slot_ref[f], held_by)
+    hit = jnp.where(held_by == entry // maxlen, 1.0, 0.0).astype(jnp.bfloat16)
+    lens = jnp.dot(
+        hit, len_ref[...].astype(jnp.float32).astype(jnp.bfloat16), preferred_element_type=jnp.float32
+    )
+    place = (lax.broadcasted_iota(jnp.int32, (span, batch), 0) % maxlen).astype(jnp.float32)
+    idx = jnp.where(place < lens, ids_ref[...], rows)
+    for o in range(owners):
+        idx_ref[o] = idx[o * each : (o + 1) * each]
+
     pl.semaphore_wait(barrier, len(near))
 
     ids_out = [
@@ -232,9 +264,12 @@
     keep_ids = pltpu.make_async_copy(idx_ref.at[t], idx_s.at[t], smem_sem.at[0])
     keep_ids.start()
 
+    loads[0].wait()
+    loads[1].wait()
     low = jnp.dot(x_ref[...], down_ref[...], preferred_element_type=jnp.float32).astype(jnp.bfloat16)
+    loads[2].wait()
     dz = (ct_ref[...].astype(jnp.float32) * x_ref[...].astype(jnp.float32)).astype(jnp.bfloat16)
-    ct = dz
+    loads[3].wait()
     dlow = lax.dot_general(
         dz, up_ref[...], (((1,), (1,)), ((), ())), preferred_element_type=jnp.float32
     ).astype(jnp.bfloat16)
@@ -243,7 +278,7 @@
         begin = block * high
         edge = begin // LANES * LANES
         stop = -(-(begin + high) // LANES) * LANES
-        up = lax.dot_general(ct[:, edge:stop], low, first, preferred_element_type=jnp.float32)
+        up = lax.dot_general(dz[:, edge:stop], low, first, preferred_element_type=jnp.float32)
         down = lax.dot_general(
             x_ref[:, edge:stop], dlow, first, preferred_element_type=jnp.float32
         )
@@ -342,19 +377,19 @@
             at = pl.ds(pl.multiple_of(c * chunk, chunk), chunk)
             wide[at, :] = stage[s % 2, at, :].astype(jnp.float32)
 
-        @pl.loop(0, owners * lines)
+        @pl.loop(0, owners * batch // group)
         def _(i):
-            src = i // lines
-            line = s * lines + i % lines
-            for u in range(per_line):
+            src = i // (batch // group)
+            line = i % (batch // group) * group
+            for u in range(group):
                 held = [
-                    wide[pl.ds(idx_s[src, line, u * maxlen + k], 1), :] for k in range(maxlen)
+                    wide[pl.ds(idx_s[src, s * maxlen + k, line + u], 1), :] for k in range(maxlen)
                 ]
                 while len(held) > 1:
                     held = [a + b for a, b in zip(held[::2], held[1::2])] + (
                         [held[-1]] if len(held) % 2 else []
                     )
-                acc[pl.ds(i * per_line + u, 1), :] = held[0]
+                acc[pl.ds(i * group + u, 1), :] = held[0]
 
         for n, at in enumerate(checkpoints):
             if at == s:
@@ -376,7 +411,9 @@
     total = part[t, z, x].astype(jnp.float32)
     for d in range(1, zs):
         total += z_in[d - 1].astype(jnp.float32)
-    grad_ref[...] = total
+    total = total.T
+    grad_up_ref[...] = total[:cols]
+    grad_down_ref[...] = total[cols:]
     for copy in returns:
         copy.wait()
     for f in range(slot_ref.shape[0]):
@@ -384,7 +421,9 @@
         emb_ref[:, f * width : (f + 1) * width] = got[lax.div(s, slots), lax.rem(s, slots)]
 
 
-def fused_step(idx, slot_of_table, tables, cross_input, cotangent, up_weight, down_weight, maxlen, factor):
+def fused_step(
+    next_ids, next_lengths, slot_of_table, tables, cross_input, cotangent, up_weight, down_weight, maxlen, factor
+):
     groups, owners = lax.axis_size("grp"), lax.axis_size("tbl")
     slots, rows, width = tables.shape
     batch, depth = cross_input.shape
@@ -392,27 +431,37 @@
     split = (high // 2 + 15) // 16 * 16
     sems = pltpu.SemaphoreType.DMA
     bf16 = jnp.bfloat16
+    any_space = pl.BlockSpec(memory_space=pl.ANY)
+    idx_shape = (owners, next_ids.shape[1] // owners, batch)
+    half = down_weight.shape[1] // owners
     vmem = pl.BlockSpec(memory_space=pltpu.VMEM)
     checkpoints = (0, min(3, slots - 1), min(5, slots - 1))
     return pl.pallas_call(
         functools.partial(step_kernel, maxlen, factor, split, checkpoints),
         out_shape=(
             jax.ShapeDtypeStruct((batch, slot_of_table.shape[0] * width), bf16),
-            jax.ShapeDtypeStruct((high, LANES), jnp.float32),
+            jax.ShapeDtypeStruct((half, high), jnp.float32),
+            jax.ShapeDtypeStruct((half, high), jnp.float32),
         ),
         in_specs=[
             vmem,
+            vmem,
             pl.BlockSpec(memory_space=pltpu.SMEM),
-            pl.BlockSpec(memory_space=pl.ANY),
-            vmem,
-            vmem,
-            vmem,
-            vmem,
+            any_space,
+            any_space,
+            any_space,
+            any_space,
+            any_space,
         ],
-        out_specs=(vmem, vmem),
+        out_specs=(vmem, vmem, vmem),
         scratch_shapes=[
-            pltpu.VMEM(idx.shape, jnp.int32),
-            pltpu.SMEM(idx.shape, jnp.int32),
+            pltpu.VMEM(cross_input.shape, bf16),
+            pltpu.VMEM(cotangent.shape, bf16),
+            pltpu.VMEM(up_weight.shape, bf16),
+            pltpu.VMEM(down_weight.shape, bf16),
+            pltpu.VMEM(idx_shape, jnp.int32),
+            pltpu.VMEM(idx_shape, jnp.int32),
+            pltpu.SMEM(idx_shape, jnp.int32),
             pltpu.VMEM((owners, zs, 2, high, LANES), bf16),
             pltpu.VMEM((2, zs, 2, high, LANES), bf16),
             pltpu.VMEM((zs, 2, split, LANES), bf16),
@@ -433,12 +482,22 @@
             sems((2, 2)),
             sems((2, max(zs - 1, 1))),
             sems((2, slots * (owners - 1))),
+            sems((4,)),
         ],
         compiler_params=pltpu.CompilerParams(
             collective_id=0, has_side_effects=True, vmem_limit_bytes=56 << 20
         ),
         name="fused_step",
-    )(idx, slot_of_table, tables, cross_input, cotangent, up_weight, down_weight)
+    )(
+        next_ids.T,
+        next_lengths.T,
+        slot_of_table,
+        tables,
+        cross_input,
+        cotangent,
+        up_weight,
+        down_weight,
+    )
 
 
 def on_device(
@@ -448,7 +507,9 @@
     batch, depth = cross_input.shape
     rank = down_weight.shape[1]
     slots, rows, _ = tables.shape
-    if owners != 4 or groups % 2 or depth % (16 * groups) or rank * 2 != owners * LANES:
+    maxlen = next_ids.shape[1] // (slots * owners)
+    fits = owners == 4 and groups % 2 == 0 and depth % (16 * groups) == 0 and batch % 16 == 0
+    if not fits or rank * 2 != owners * LANES or slots * maxlen % 8 or batch != LANES:
         return plain(
             next_ids,
             next_lengths,
@@ -459,14 +520,20 @@
             up_weight,
             down_weight,
         )
-    maxlen = next_ids.shape[1] // (slots * owners)
     factor = 1.0 / math.sqrt(batch * groups * owners)
-    idx = bag_rows(next_ids, next_lengths, slot_of_table, slots, owners, rows)
-    next_embedded, grads = fused_step(
-        idx, slot_of_table, tables, cross_input, cotangent, up_weight, down_weight, maxlen, factor
-    )
-    half = LANES // 2
-    return next_embedded, grads[:, :half].T, grads[:, half:]
+    next_embedded, grad_up, grad_down = fused_step(
+        next_ids,
+        next_lengths,
+        slot_of_table,
+        tables,
+        cross_input,
+        cotangent,
+        up_weight,
+        down_weight,
+        maxlen,
+        factor,
+    )
+    return next_embedded, grad_up, grad_down.T
 
 
 def solution(mesh):

time: 62 us -> 75.3 us (1.21)
  Pallas kernels: 49.8 us -> 71 us
  local copies, waits for them, and re-layouts: 7.87 us -> 3.47 us
  other arithmetic: 3.47 us -> 0 us
    pallas_call x1, Pallas kernels: 49.8 us -> 71 us  [fused_step(): pl.pallas_call(functools.partial(step_kernel, maxlen, factor, split, chec...]
    reshape x2 -> x0, local copies, waits for them, and re-layouts: 4.18 us -> none  [the longest x1 2.71 us: bag_rows(): idx = jnp.where(keep, next_ids.reshape(batch, slots_all, maxlen), rows)]
    transpose x1 -> x0, other arithmetic: 1.85 us -> none  [bag_rows(): idx.transpose(1, 0, 2)]
    slice x1 -> x0, local copies, waits for them, and re-layouts: 1.23 us -> none  [on_device(): return (next_embedded, grads[:, :half].T, grads[:, half:])]
    unnamed x5 -> x7, local copies, waits for them, and re-layouts: 2.45 us -> 3.47 us
    reduce_sum x1 -> x0, other arithmetic: 0.89 us -> none  [bag_rows(): slot_lengths = jnp.sum(next_lengths[:, :, None] * hit[None, :, :], axis=1)]
where the time goes in v3:
time: 75.3 us; the launch traced here: 75.2 us
  Pallas kernels  71 us (94%)
  local copies, waits for them, and re-layouts  3.47 us (5%)
    pallas_call x1, Pallas kernels, fused_step(): pl.pallas_call(functools.partial(step_kernel, maxlen, factor, split, chec...  71 us
    unnamed x7, local copies, waits for them, and re-layouts  3.47 us

profile of v3, /device:TPU:0, one launch (start us, length us, event | category | flops | bytes accessed | tf_op | source)
XLA Modules:
  0.0 75.2 jit_solution(15357729944986771822)
XLA Ops:
  0.6 71.0 %fused_step.1 = (bf16[128,3328]{1,0:T(8,128)(2,1)}, f32[64,432]{1,0:T(8,128)}, f32[64,432]{1,0:T(8,128)}) custom-call(s32[224,128]{1,0:T(8,128)} %bitcast.4, s32[26,128]{1,0:T(8,128)} %bitcast.5, s32[26]{0:T(128)} %slot_ref.1, bf16[7,6144,128]{2,1,0:T(8,128)(2,1)} %tab_ref.1, bf16[128,3456]{1,0:T(8,128)(2,1)} %x_hbm.1, bf16[128,3456]{1,0:T(8,128)(2,1)} %ct_hbm.1, ...), custom_call_target="tpu_custom_call" | custom-call | tf_op jit(solution)/shard_map/fused_step/pallas_call | solution.py:439
  71.7 0.0 copy-start.1
  71.7 0.0 copy-start
  71.7 2.2 %copy.14 = bf16[128,3328]{1,0:T(8,128)(2,1)} copy(bf16[128,3328]{1,0:T(8,128)(2,1)} %get-tuple-element.12) | data formatting | bytes 1703936
  73.9 0.0 copy-done.1
  73.9 0.7 copy.15
  74.5 0.0 copy-done
  74.5 0.7 copy.16
Async XLA Ops:
  71.7 2.2 %copy-start.1 = (f32[64,432]{1,0:T(8,128)S(1)}, f32[64,432]{1,0:T(8,128)}, u32[]{:S(2)}) copy-start(f32[64,432]{1,0:T(8,128)} %get-tuple-element.13) | copy-start | bytes 331780
  71.7 2.8 %copy-start = (f32[64,432]{1,0:T(8,128)S(1)}, f32[64,432]{1,0:T(8,128)}, u32[]{:S(2)}) copy-start(f32[64,432]{1,0:T(8,128)} %get-tuple-element.8) | copy-start | bytes 331780

commit v4 on v3

--- a/solution.py
+++ b/solution.py
@@ -170,6 +170,7 @@
     down_ref,
     idx_ref,
     idx_in,
+    turned,
     idx_s,
     part,
     c_in,
@@ -261,8 +262,6 @@
     ]
     for copy in ids_out:
         copy.start()
-    keep_ids = pltpu.make_async_copy(idx_ref.at[t], idx_s.at[t], smem_sem.at[0])
-    keep_ids.start()
 
     loads[0].wait()
     loads[1].wait()
@@ -298,12 +297,12 @@
 
     for copy in ids_out:
         copy.wait()
-    keep_ids.wait()
+    idx_in[t] = idx_ref[t]
+    for o in range(owners):
+        turned[o] = jnp.zeros((batch, LANES), jnp.int32)
+        turned[o, :, :each] = idx_in[o].T
     got_ids = [
-        pltpu.make_async_copy(
-            idx_in.at[(t + d) % owners], idx_s.at[(t + d) % owners], smem_sem.at[d]
-        )
-        for d in range(1, owners)
+        pltpu.make_async_copy(turned.at[o], idx_s.at[o], smem_sem.at[o]) for o in range(owners)
     ]
     for copy in got_ids:
         copy.start()
@@ -383,7 +382,7 @@
             line = i % (batch // group) * group
             for u in range(group):
                 held = [
-                    wide[pl.ds(idx_s[src, s * maxlen + k, line + u], 1), :] for k in range(maxlen)
+                    wide[pl.ds(idx_s[src, line + u, s * maxlen + k], 1), :] for k in range(maxlen)
                 ]
                 while len(held) > 1:
                     held = [a + b for a, b in zip(held[::2], held[1::2])] + (
@@ -461,7 +460,8 @@
             pltpu.VMEM(down_weight.shape, bf16),
             pltpu.VMEM(idx_shape, jnp.int32),
             pltpu.VMEM(idx_shape, jnp.int32),
-            pltpu.SMEM(idx_shape, jnp.int32),
+            pltpu.VMEM((owners, batch, LANES), jnp.int32),
+            pltpu.SMEM((owners, batch, LANES), jnp.int32),
             pltpu.VMEM((owners, zs, 2, high, LANES), bf16),
             pltpu.VMEM((2, zs, 2, high, LANES), bf16),
             pltpu.VMEM((zs, 2, split, LANES), bf16),
@@ -509,7 +509,7 @@
     slots, rows, _ = tables.shape
     maxlen = next_ids.shape[1] // (slots * owners)
     fits = owners == 4 and groups % 2 == 0 and depth % (16 * groups) == 0 and batch % 16 == 0
-    if not fits or rank * 2 != owners * LANES or slots * maxlen % 8 or batch != LANES:
+    if not fits or rank * 2 != owners * LANES or slots * maxlen % 8 or slots * maxlen > LANES or batch != LANES:
         return plain(
             next_ids,
             next_lengths,

time: 75.3 us -> 57.6 us (0.76)
  Pallas kernels: 71 us -> 53.3 us
    pallas_call x1, Pallas kernels: 71 us -> 53.3 us  [fused_step(): pl.pallas_call(functools.partial(step_kernel, maxlen, factor, split, chec...]
where the time goes in v4:
time: 57.6 us; the launch traced here: 57.4 us
  Pallas kernels  53.3 us (93%)
  local copies, waits for them, and re-layouts  3.47 us (6%)
  between operations  0.66 us (1%)
    pallas_call x1, Pallas kernels, fused_step(): pl.pallas_call(functools.partial(step_kernel, maxlen, factor, split, chec...  53.3 us
    unnamed x7, local copies, waits for them, and re-layouts  3.47 us

profile of v4, /device:TPU:0, one launch (start us, length us, event | category | flops | bytes accessed | tf_op | source)
XLA Modules:
  0.0 57.4 jit_solution(1370184768881238736)
XLA Ops:
  0.6 53.3 %fused_step.1 = (bf16[128,3328]{1,0:T(8,128)(2,1)}, f32[64,432]{1,0:T(8,128)}, f32[64,432]{1,0:T(8,128)}) custom-call(s32[224,128]{1,0:T(8,128)} %bitcast.4, s32[26,128]{1,0:T(8,128)} %bitcast.5, s32[26]{0:T(128)} %slot_ref.1, bf16[7,6144,128]{2,1,0:T(8,128)(2,1)} %tab_ref.1, bf16[128,3456]{1,0:T(8,128)(2,1)} %x_hbm.1, bf16[128,3456]{1,0:T(8,128)(2,1)} %ct_hbm.1, ...), custom_call_target="tpu_custom_call" | custom-call | tf_op jit(solution)/shard_map/fused_step/pallas_call | solution.py:438
  53.9 0.0 copy-start.1
  54.0 0.0 copy-start
  54.0 2.2 %copy.14 = bf16[128,3328]{1,0:T(8,128)(2,1)} copy(bf16[128,3328]{1,0:T(8,128)(2,1)} %get-tuple-element.12) | data formatting | bytes 1703936
  56.1 0.0 copy-done.1
  56.1 0.7 %copy.15 = f32[64,432]{1,0:T(8,128)} copy(f32[64,432]{1,0:T(8,128)S(1)} %copy-done.1) | data formatting | bytes 221184
  56.8 0.0 copy-done
  56.8 0.7 %copy.16 = f32[432,64]{0,1:T(8,128)} copy(f32[432,64]{0,1:T(8,128)S(1)} %bitcast.3) | data formatting | bytes 221184
Async XLA Ops:
  53.9 2.2 %copy-start.1 = (f32[64,432]{1,0:T(8,128)S(1)}, f32[64,432]{1,0:T(8,128)}, u32[]{:S(2)}) copy-start(f32[64,432]{1,0:T(8,128)} %get-tuple-element.13) | copy-start | bytes 331780
  54.0 2.8 %copy-start = (f32[64,432]{1,0:T(8,128)S(1)}, f32[64,432]{1,0:T(8,128)}, u32[]{:S(2)}) copy-start(f32[64,432]{1,0:T(8,128)} %get-tuple-element.8) | copy-start | bytes 331780

commit v5 on v4

--- a/solution.py
+++ b/solution.py
@@ -199,8 +199,8 @@
     batch = x_ref.shape[0]
     rank = down_ref.shape[1]
     cols = rank // owners
-    group = 16
-    chunk = 256
+    group = 32
+    chunk = 1024 if rows % 1024 == 0 else 256
     g, t = lax.axis_index("grp"), lax.axis_index("tbl")
     z, x = g // 2, g % 2
     core = t + 1 - 2 * (t % 2)
@@ -302,7 +302,10 @@
         turned[o] = jnp.zeros((batch, LANES), jnp.int32)
         turned[o, :, :each] = idx_in[o].T
     got_ids = [
-        pltpu.make_async_copy(turned.at[o], idx_s.at[o], smem_sem.at[o]) for o in range(owners)
+        pltpu.make_async_copy(
+            turned.at[o], idx_s.at[pl.ds(o * batch, batch)], smem_sem.at[o]
+        )
+        for o in range(owners)
     ]
     for copy in got_ids:
         copy.start()
@@ -378,11 +381,9 @@
 
         @pl.loop(0, owners * batch // group)
         def _(i):
-            src = i // (batch // group)
-            line = i % (batch // group) * group
             for u in range(group):
                 held = [
-                    wide[pl.ds(idx_s[src, line + u, s * maxlen + k], 1), :] for k in range(maxlen)
+                    wide[pl.ds(idx_s[i * group + u, s * maxlen + k], 1), :] for k in range(maxlen)
                 ]
                 while len(held) > 1:
                     held = [a + b for a, b in zip(held[::2], held[1::2])] + (
@@ -461,7 +462,7 @@
             pltpu.VMEM(idx_shape, jnp.int32),
             pltpu.VMEM(idx_shape, jnp.int32),
             pltpu.VMEM((owners, batch, LANES), jnp.int32),
-            pltpu.SMEM((owners, batch, LANES), jnp.int32),
+            pltpu.SMEM((owners * batch, LANES), jnp.int32),
             pltpu.VMEM((owners, zs, 2, high, LANES), bf16),
             pltpu.VMEM((2, zs, 2, high, LANES), bf16),
             pltpu.VMEM((zs, 2, split, LANES), bf16),

time: 57.6 us -> 55.2 us (0.958)
  Pallas kernels: 53.3 us -> 50.9 us
    pallas_call x1, Pallas kernels: 53.3 us -> 50.9 us  [fused_step(): pl.pallas_call(functools.partial(step_kernel, maxlen, factor, split, chec...]
where the time goes in v5:
time: 55.2 us; the launch traced here: 55.1 us
  Pallas kernels  50.9 us (92%)
  local copies, waits for them, and re-layouts  3.47 us (6%)
  between operations  0.66 us (1%)
    pallas_call x1, Pallas kernels, fused_step(): pl.pallas_call(functools.partial(step_kernel, maxlen, factor, split, chec...  50.9 us
    unnamed x7, local copies, waits for them, and re-layouts  3.47 us

profile of v5, /device:TPU:0, one launch (start us, length us, event | category | flops | bytes accessed | tf_op | source)
XLA Modules:
  0.0 55.1 jit_solution(12863984214265374937)
XLA Ops:
  0.6 50.9 %fused_step.1 = (bf16[128,3328]{1,0:T(8,128)(2,1)}, f32[64,432]{1,0:T(8,128)}, f32[64,432]{1,0:T(8,128)}) custom-call(s32[224,128]{1,0:T(8,128)} %bitcast.4, s32[26,128]{1,0:T(8,128)} %bitcast.5, s32[26]{0:T(128)} %slot_ref.1, bf16[7,6144,128]{2,1,0:T(8,128)(2,1)} %tab_ref.1, bf16[128,3456]{1,0:T(8,128)(2,1)} %x_hbm.1, bf16[128,3456]{1,0:T(8,128)(2,1)} %ct_hbm.1, ...), custom_call_target="tpu_custom_call" | custom-call | tf_op jit(solution)/shard_map/fused_step/pallas_call | solution.py:439
  51.6 0.0 copy-start.1
  51.6 0.0 copy-start
  51.6 2.2 %copy.14 = bf16[128,3328]{1,0:T(8,128)(2,1)} copy(bf16[128,3328]{1,0:T(8,128)(2,1)} %get-tuple-element.12) | data formatting | bytes 1703936
  53.8 0.0 copy-done.1
  53.8 0.7 %copy.15 = f32[64,432]{1,0:T(8,128)} copy(f32[64,432]{1,0:T(8,128)S(1)} %copy-done.1) | data formatting | bytes 221184
  54.4 0.0 copy-done
  54.4 0.7 %copy.16 = f32[432,64]{0,1:T(8,128)} copy(f32[432,64]{0,1:T(8,128)S(1)} %bitcast.3) | data formatting | bytes 221184
Async XLA Ops:
  51.6 2.2 %copy-start.1 = (f32[64,432]{1,0:T(8,128)S(1)}, f32[64,432]{1,0:T(8,128)}, u32[]{:S(2)}) copy-start(f32[64,432]{1,0:T(8,128)} %get-tuple-element.13) | copy-start | bytes 331780
  51.6 2.8 %copy-start = (f32[64,432]{1,0:T(8,128)S(1)}, f32[64,432]{1,0:T(8,128)}, u32[]{:S(2)}) copy-start(f32[64,432]{1,0:T(8,128)} %get-tuple-element.8) | copy-start | bytes 331780
